TPU v7x, 32 devices: a whole 2x2x4 slice. The times are simulated.
32 devices in a mesh: role: 2 (over core), dev: 16 (over z, y, x).
Axes of the slice: x: 2, y: 2, z: 4, core: 2. Of those that a mesh axis runs over, the one named last changes fastest.
Arguments:
- table_rows: bfloat16 [32, 2048, 128], P('dev'), may hold values from -6 to 6
- piece_table: int32 [32], replicated, may hold values from 0 to 25, as said below
- bag_rows: int32 [32, 8192], P('dev'), may hold values from 0 to 2047
- bag_of: int32 [32, 8192], P('dev'), may hold values from 0 to 4095, never falling along the last dimension, each value on 1 to 8 neighbouring positions
- bag_weight: bfloat16 [32, 8192], P('dev'), may hold values from 0.25 to 2
- dense_input: bfloat16 [4096, 128], P('dev'), may hold values from -6 to 6
- labels: float32 [4096], P('dev'), may hold values from 0 to 1
- cross_u: bfloat16 [3456, 512], replicated, may hold values from -0.109375 to 0.109375
- cross_v: bfloat16 [512, 3456], replicated, may hold values from -0.25 to 0.25
- cross_bias: float32 [3456], replicated, may hold values from -3 to 3
- top_w1: bfloat16 [3456, 1024], replicated, may hold values from -0.109375 to 0.109375
- top_b1: float32 [1024], replicated, may hold values from -3 to 3
- out_w: bfloat16 [1024], replicated, may hold values from -0.375 to 0.375
Outputs:
- piece_grads: bfloat16 [16, 256, 32, 128], P(None, 'role', 'dev')
Inputs may be any that keep to these rules, and one draw needn't show every extreme that they name: `piece_table`: every one of the 26 tables owns one piece or more. `bag_of`: in each piece the bag numbers never fall along the lookups, and every sample has 1 to 8 lookups in every piece.
All inputs are finite; a program needn't handle non-finite values.
Results may differ from a plain program's by a relative error of at most 0.012.
The roundings to bfloat16 on the way count: a program that leaves them out, or rounds other values in their place, can miss the bound.
Values may be sent and summed in bfloat16 or wider, within the bound.
A program may use at most 128 MiB of HBM per device.

v0:
```python
import jax
import jax.numpy as jnp
from jax import lax
from jax.experimental import pallas as pl
from jax.experimental.pallas import tpu as pltpu
from jax.sharding import PartitionSpec as P

LANES = 128
WINDOW = 384
LOW = 256
CHUNKS = 2
NT = (((1,), (1,)), ((), ()))
NN = (((1,), (0,)), ((), ()))


def dot(a, b, dims=NN):
    return lax.dot_general(a, b, dims, preferred_element_type=jnp.float32)


def pool_kernel(
    owner_ref, first_ref, last_ref, table_ref, rows_ref, bags_ref, scale_ref,
    out_ref, lead_ref, spare_ref, spare_owner_ref, flipped, scale_wide,
):
    blocks, pieces, half, width = out_ref.shape
    length = table_ref.shape[1]
    total = rows_ref.shape[1]
    groups = length // LOW
    role = lax.axis_index("role")

    @pl.loop(0, lead_ref.shape[0])
    def _(t):
        lead_ref[t] = -1

    @pl.loop(0, spare_ref.shape[0])
    def _(e):
        spare_ref[e] = 0
        spare_owner_ref[e] = -1

    def assign(p, used):
        t = owner_ref[p]
        again = lead_ref[t] >= 0

        @pl.when(again)
        def _():
            spare_ref[used] = p
            spare_owner_ref[used] = t

        @pl.when(jnp.logical_not(again))
        def _():
            lead_ref[t] = p

        return used + again.astype(jnp.int32)

    lax.fori_loop(0, owner_ref.shape[0], assign, jnp.int32(0))
    scale_wide[...] = scale_ref[...].astype(jnp.float32)
    for p in range(pieces):
        for g in range(groups):
            flipped[p, g * width : (g + 1) * width, :] = (
                table_ref[p, g * LOW : (g + 1) * LOW, :].astype(jnp.float32).T.astype(jnp.bfloat16)
            )
    low_ids = lax.broadcasted_iota(jnp.int32, (LOW, WINDOW), 0)
    bag_ids = lax.broadcasted_iota(jnp.int32, (half, WINDOW), 0)
    places = lax.broadcasted_iota(jnp.int32, (1, WINDOW), 1)

    def window(p, base, begin, first_bag):
        start = pl.multiple_of(jnp.minimum(begin, total - WINDOW), LANES)
        span = pl.ds(start, WINDOW)
        ids = rows_ref[pl.ds(p, 1), span]
        bags = bags_ref[pl.ds(p, 1), span] - first_bag
        bags = jnp.where(places + start >= begin, bags, -1)
        scale = scale_wide[pl.ds(p, 1), span]
        low, high = ids % LOW, ids // LOW
        hot = jnp.where(low_ids == low, 1.0, 0.0).astype(jnp.bfloat16)
        picked = dot(flipped[p, :width, :], hot)
        for g in range(1, groups):
            picked = jnp.where(high == g, dot(flipped[p, g * width : (g + 1) * width, :], hot), picked)
        spread = jnp.where(bag_ids == bags, scale, 0.0).astype(jnp.bfloat16)
        return dot(spread, picked.astype(jnp.bfloat16), NT)

    @pl.loop(0, blocks)
    def _(k):
        first_bag = (2 * k + role) * half
        bases = [first_ref[p, k] // LANES * LANES for p in range(pieces)]
        sums = [window(p, bases[p], bases[p], first_bag) for p in range(pieces)]
        for p in range(pieces):
            out_ref[k, p] = sums[p].astype(jnp.bfloat16)
        for p in range(pieces):
            count = (last_ref[p, k] - bases[p] + WINDOW - 1) // WINDOW

            @pl.when(count > 1)
            def _():
                def more(j, acc):
                    return acc + window(p, bases[p], bases[p] + j * WINDOW, first_bag)

                first = window(p, bases[p], bases[p], first_bag)
                out_ref[k, p] = lax.fori_loop(1, count, more, first).astype(jnp.bfloat16)


def pool(piece_table, table_rows, bag_rows, bag_of, bag_weight, half, blocks, tables):
    pieces, length, width = table_rows.shape
    role = lax.axis_index("role")
    edges = (2 * jnp.arange(blocks, dtype=jnp.int32) + role) * half
    first = jnp.sum((bag_of[:, None, :] < edges[None, :, None]).astype(jnp.int32), axis=2)
    last = jnp.sum((bag_of[:, None, :] < edges[None, :, None] + half).astype(jnp.int32), axis=2)
    spares = max(1, piece_table.shape[0] - tables)
    vmem = pl.BlockSpec(memory_space=pltpu.VMEM)
    smem = pl.BlockSpec(memory_space=pltpu.SMEM)
    return pl.pallas_call(
        pool_kernel,
        out_shape=[
            jax.ShapeDtypeStruct((blocks, pieces, half, width), jnp.bfloat16),
            jax.ShapeDtypeStruct((tables,), jnp.int32),
            jax.ShapeDtypeStruct((spares,), jnp.int32),
            jax.ShapeDtypeStruct((spares,), jnp.int32),
        ],
        in_specs=[smem, smem, smem, vmem, vmem, vmem, vmem],
        out_specs=[vmem, smem, smem, smem],
        scratch_shapes=[
            pltpu.VMEM((pieces, length // LOW * width, LOW), jnp.bfloat16),
            pltpu.VMEM(bag_weight.shape, jnp.float32),
        ],
        compiler_params=pltpu.CompilerParams(vmem_limit_bytes=40 * 1024 * 1024),
    )(piece_table, first, last, table_rows, bag_rows, bag_of, bag_weight)


def dense_kernel(
    owner_ref, lead_ref, spare_ref, spare_owner_ref, pooled_ref, dense_ref, label_ref, bias_ref, b1_ref,
    out_w_ref, u_hbm, v_hbm, w_hbm, out_ref,
    u_ref, v_ref, w_ref, feats, crossed, mixed_grad, grads, arrived, outgoing,
    sems, there_send, there_recv, back_send, back_recv,
):
    devices, local_pieces, half, width = pooled_ref.shape
    pieces = devices * local_pieces
    rows, wide = feats.shape
    tables = wide // width - 1
    role = lax.axis_index("role")
    me = lax.axis_index("dev")
    load_u = pltpu.make_async_copy(u_hbm, u_ref, sems.at[0])
    load_v = pltpu.make_async_copy(v_hbm, v_ref, sems.at[1])
    load_w = pltpu.make_async_copy(w_hbm, w_ref, sems.at[2])

    barrier = pltpu.get_barrier_semaphore()

    @pl.loop(1, devices)
    def _(s):
        pl.semaphore_signal(
            barrier, inc=1, device_id={"dev": (me + s) % devices}, device_id_type=pl.DeviceIdType.MESH
        )

    load_u.start()
    load_v.start()
    load_w.start()
    pl.semaphore_wait(barrier, devices - 1)

    def there(c, s):
        peer = (me + s) % devices
        return pltpu.make_async_remote_copy(
            src_ref=pooled_ref.at[peer, :, c * rows : (c + 1) * rows, :],
            dst_ref=arrived[c].at[me],
            send_sem=there_send.at[c, s],
            recv_sem=there_recv.at[c, s],
            device_id={"dev": peer},
            device_id_type=pl.DeviceIdType.MESH,
        )

    def back(c, s):
        peer = (me + s) % devices
        return pltpu.make_async_remote_copy(
            src_ref=outgoing[c].at[peer],
            dst_ref=out_ref.at[me, :, c * rows : (c + 1) * rows, :],
            send_sem=back_send.at[c, s],
            recv_sem=back_recv.at[c, s],
            device_id={"dev": peer},
            device_id_type=pl.DeviceIdType.MESH,
        )

    for c in range(CHUNKS):

        @pl.loop(1, devices)
        def _(s):
            there(c, s).start()

    for c in range(CHUNKS):
        arrived[c][me] = pooled_ref[me, :, c * rows : (c + 1) * rows, :]

    step = next(n for n in (3 * width, width) if wide % n == 0)
    parts = [slice(i, i + step) for i in range(0, wide, step)]
    out_weight = out_w_ref[...].astype(jnp.float32)
    row_at = lax.broadcasted_iota(jnp.int32, (rows, rows), 0)
    column_at = lax.broadcasted_iota(jnp.int32, (rows, rows), 1)
    spares = pieces - tables

    for c in range(CHUNKS):
        feats[:, :width] = dense_ref[pl.ds(pl.multiple_of(role * half + c * rows, rows), rows), :].astype(jnp.float32)

        @pl.loop(1, devices)
        def _(s):
            there(c, s).wait_recv()

        def piece(index):
            return arrived[c][index // local_pieces, index % local_pieces].astype(jnp.float32)

        @pl.loop(0, tables)
        def _(t):
            def add(e, acc):
                return acc + piece(spare_ref[e]) * jnp.where(spare_owner_ref[e] == t, 1.0, 0.0)

            acc = piece(lead_ref[t])
            if spares <= 16:
                for e in range(spares):
                    acc = add(e, acc)
            else:
                acc = lax.fori_loop(0, spares, add, acc)
            feats[:, pl.ds(pl.multiple_of((t + 1) * width, width), width)] = acc

        if c == 0:
            load_u.wait()
        low_rank = dot(feats[...].astype(jnp.bfloat16), u_ref[...]).astype(jnp.bfloat16)
        if c == 0:
            load_v.wait()
            load_w.wait()
        pre_act = b1_ref[...]
        for part in parts:
            cross_out = dot(low_rank, v_ref[:, part]) + bias_ref[:, part]
            crossed[:, part] = cross_out
            own = feats[:, part]
            pre_act = pre_act + dot((own * cross_out + own).astype(jnp.bfloat16), w_ref[part, :])
        sig_act = jax.nn.sigmoid(pre_act)
        logits = jnp.sum(pre_act * sig_act * out_weight, axis=1, keepdims=True)
        labels = jnp.sum(
            jnp.where(row_at == column_at, label_ref[pl.ds(role * CHUNKS + c, 1), :], 0.0),
            axis=1,
            keepdims=True,
        )
        grad_logit = jax.nn.sigmoid(logits) - labels
        slope = sig_act * (1.0 + pre_act * (1.0 - sig_act))
        grad_act = (grad_logit * out_weight * slope).astype(jnp.bfloat16)
        grad_low = jnp.zeros((rows, u_ref.shape[1]), jnp.float32)
        for part in parts:
            grad_mixed = dot(grad_act, w_ref[part, :], NT)
            grad_cross = (grad_mixed * feats[:, part]).astype(jnp.bfloat16)
            mixed_grad[:, part] = grad_mixed * (crossed[:, part] + 1.0)
            grad_low = grad_low + dot(grad_cross, v_ref[:, part], NT)
        grad_low = grad_low.astype(jnp.bfloat16)
        for part in parts:
            total = (mixed_grad[:, part] + dot(grad_low, u_ref[part, :], NT)).astype(jnp.bfloat16)
            for i in range(step // width):
                grads[part.start // width + i] = total[:, i * width : (i + 1) * width]

        @pl.loop(0, devices)
        def _(d):
            for i in range(local_pieces):
                outgoing[c][d, i] = grads[owner_ref[d * local_pieces + i] + 1]

        @pl.loop(1, devices)
        def _(s):
            back(c, s).start()

        out_ref[me, :, c * rows : (c + 1) * rows, :] = outgoing[c][me]

    for c in range(CHUNKS):

        @pl.loop(1, devices)
        def _(s):
            there(c, s).wait_send()
            back(c, s).wait_send()
            back(c, s).wait_recv()


def dense(chosen, pooled, piece_table, dense_input, labels, cross_u, cross_v, cross_bias, top_w1, top_b1, out_w):
    devices, local_pieces, half, width = pooled.shape
    rows = half // CHUNKS
    wide = cross_u.shape[0]
    vmem = pl.BlockSpec(memory_space=pltpu.VMEM)
    smem = pl.BlockSpec(memory_space=pltpu.SMEM)
    anywhere = pl.BlockSpec(memory_space=pl.ANY)
    block = pltpu.VMEM((devices, local_pieces, rows, width), jnp.bfloat16)
    return pl.pallas_call(
        dense_kernel,
        out_shape=jax.ShapeDtypeStruct(pooled.shape, jnp.bfloat16),
        in_specs=[smem] * 4 + [vmem] * 6 + [anywhere] * 3,
        out_specs=vmem,
        scratch_shapes=[
            pltpu.VMEM(cross_u.shape, jnp.bfloat16),
            pltpu.VMEM(cross_v.shape, jnp.bfloat16),
            pltpu.VMEM(top_w1.shape, jnp.bfloat16),
            pltpu.VMEM((rows, wide), jnp.float32),
            pltpu.VMEM((rows, wide), jnp.float32),
            pltpu.VMEM((rows, wide), jnp.float32),
            pltpu.VMEM((wide // width, rows, width), jnp.bfloat16),
            [block] * CHUNKS,
            [block] * CHUNKS,
            pltpu.SemaphoreType.DMA((3,)),
        ]
        + [pltpu.SemaphoreType.DMA((CHUNKS, devices))] * 4,
        compiler_params=pltpu.CompilerParams(
            vmem_limit_bytes=56 * 1024 * 1024, collective_id=0, has_side_effects=True
        ),
    )(
        piece_table, *chosen, pooled, dense_input, labels.reshape(2 * CHUNKS, rows), cross_bias[None],
        top_b1[None], out_w[None], cross_u, cross_v, top_w1,
    )


def local(
    table_rows, piece_table, bag_rows, bag_of, bag_weight, dense_input, labels,
    cross_u, cross_v, cross_bias, top_w1, top_b1, out_w,
):
    devices = lax.axis_size("dev")
    half = dense_input.shape[0] // 2
    tables = cross_bias.shape[0] // dense_input.shape[1] - 1
    pooled, *chosen = pool(piece_table, table_rows, bag_rows, bag_of, bag_weight, half, devices, tables)
    returned = dense(
        chosen, pooled, piece_table, dense_input, labels, cross_u, cross_v, cross_bias, top_w1, top_b1, out_w
    )
    return returned.transpose(0, 2, 1, 3)


def solution(mesh):
    split, whole = P("dev"), P()
    return jax.shard_map(
        local,
        mesh=mesh,
        in_specs=(split, whole, split, split, split, split, split) + (whole,) * 6,
        out_specs=P(None, "role", "dev", None),
        check_vma=False,
    )
```

profile of v0, /device:TPU:0, one launch (start us, length us, event | category | flops | bytes accessed | tf_op | source)
XLA Modules:
  0.0 99.1 jit_solution(1600378005518883055)
XLA Ops:
  0.0 1.3 %convert_reduce_fusion = (s32[2,16]{1,0:T(2,128)S(1)}, s32[2,16]{1,0:T(2,128)S(1)}) fusion(s32[2,8192]{1,0:T(2,128)} %bags_ref.1, s32[16]{0:T(128)S(1)} %get-tuple-element.16, s32[16]{0:T(128)S(1)} %get-tuple-element.15), kind=kLoop, calls=%fused_computation | loop fusion | flops 1572800 | bytes 65920 | tf_op jit(solution)/shard_map/reduce_sum | solution.py:104
  1.3 1.3 %reshape.14.label_ref = f32[4,64]{1,0:T(4,128)} reshape(f32[256]{0:T(256)} %param.19) | data formatting | bytes 2048 | tf_op jit(solution)/shard_map/reshape | solution.py:300
  2.6 1.3 %broadcast_in_dim.15.out_w_ref = bf16[1,1024]{1,0:T(2,128)(2,1)} reshape(bf16[1024]{0:T(1024)(128)(2,1)} %param.25) | data formatting | bytes 4096 | tf_op jit(solution)/shard_map/broadcast_in_dim | solution.py:301
  3.9 1.3 %broadcast_in_dim.6.bias_ref = f32[1,3456]{1,0:T(1,128)} reshape(f32[3456]{0:T(1024)} %param.22) | data formatting | bytes 27648 | tf_op jit(solution)/shard_map/broadcast_in_dim | solution.py:300
  5.2 0.0 copy-start
  5.2 1.2 %copy-done = bf16[2,2048,128]{2,1,0:T(8,128)(2,1)S(1)} copy-done((bf16[2,2048,128]{2,1,0:T(8,128)(2,1)S(1)}, bf16[2,2048,128]{2,1,0:T(8,128)(2,1)}, u32[]{:S(2)}) %copy-start) | copy-done | bytes 1048600
  6.4 0.0 copy-start.2
  6.4 0.8 copy-done.2
  7.2 0.0 copy-start.3
  7.3 0.8 copy-done.3
  8.1 0.0 copy-start.4
  8.1 0.8 copy-done.4
  8.8 0.0 copy-start.5
  8.8 0.7 copy-done.5
  9.5 21.8 %shard_map.127 = (bf16[16,2,128,128]{3,2,1,0:T(8,128)(2,1)S(1)}, s32[26]{0:T(128)S(1)}, s32[6]{0:T(128)S(1)}, s32[6]{0:T(128)S(1)}) custom-call(s32[32]{0:T(128)S(1)} %copy-done.5, s32[2,16]{1,0:T(2,128)S(1)} %get-tuple-element.14.first_ref, s32[2,16]{1,0:T(2,128)S(1)} %get-tuple-element.13.last_ref, bf16[2,2048,128]{2,1,0:T(8,128)(2,1)S(1)} %copy-done, ...), custom_call_target="tpu_custom_call" | custom-call | tf_op jit(solution)/shard_map/pallas_call | solution.py:108
  31.3 0.0 copy-start.1
  31.3 1.0 copy-done.1
  32.3 0.0 copy-start.6
  32.3 0.5 copy-done.6
  32.8 0.0 copy-start.7
  32.8 0.5 copy-done.7
  33.4 0.0 copy-start.8
  33.4 0.5 copy-done.8
  33.9 62.0 %shard_map.128 = bf16[16,2,128,128]{3,2,1,0:T(8,128)(2,1)} custom-call(s32[32]{0:T(128)} %owner_ref.3, s32[26]{0:T(128)} %copy-done.6, s32[6]{0:T(128)} %copy-done.7, s32[6]{0:T(128)} %copy-done.8, bf16[16,2,128,128]{3,2,1,0:T(8,128)(2,1)} %copy-done.1, bf16[256,128]{1,0:T(8,128)(2,1)} %dense_ref.1, f32[4,64]{1,0:T(4,128)} %reshape.14.label_ref, ...), custom_call_target="tpu_custom_call" | custom-call | tf_op jit(solution)/shard_map/pallas_call | solution.py:278
  95.8 3.3 %copy.15 = bf16[16,128,2,128]{3,2,1,0:T(2,128)(2,1)} copy(bf16[16,128,2,128]{3,1,2,0:T(8,128)(2,1)} %bitcast.2) | data formatting | bytes 2097152 | tf_op jit(solution)/shard_map/transpose | solution.py:316
  (1 shorter events, 0.0 us)
Async XLA Ops:
  5.2 1.2 %copy-start = (bf16[2,2048,128]{2,1,0:T(8,128)(2,1)S(1)}, bf16[2,2048,128]{2,1,0:T(8,128)(2,1)}, u32[]{:S(2)}) copy-start(bf16[2,2048,128]{2,1,0:T(8,128)(2,1)} %table_ref.1) | copy-start | bytes 3145732
  6.4 0.8 copy-start.2
  7.2 0.8 copy-start.3
  8.1 0.8 copy-start.4
  8.8 0.7 copy-start.5
  31.3 1.0 copy-start.1
  32.3 0.5 copy-start.6
  32.8 0.5 copy-start.7
  33.4 0.5 copy-start.8
where the time goes:
time: 97.8 us; the launch traced here: 99.1 us
  Pallas kernels  83.8 us (86%)
  local copies, waits for them, and re-layouts  14.1 us (14%)
  other arithmetic  1.26 us (1%)
    pallas_call x1, Pallas kernels, dense(): pl.pallas_call(dense_kernel, out_shape=jax.ShapeDtypeStruct(pooled.shape,...  62 us
    pallas_call x1, Pallas kernels, pool(): pl.pallas_call(pool_kernel, out_shape=[jax.ShapeDtypeStruct((blocks, piec...  21.8 us
    unnamed x18, local copies, waits for them, and re-layouts  6.85 us
    transpose x1, local copies, waits for them, and re-layouts, local(): return returned.transpose(0, 2, 1, 3)  3.28 us

commit v1 on v0

--- a/solution.py
+++ b/solution.py
@@ -185,9 +185,9 @@
 
     step = next(n for n in (3 * width, width) if wide % n == 0)
     parts = [slice(i, i + step) for i in range(0, wide, step)]
-    out_weight = out_w_ref[...].astype(jnp.float32)
-    row_at = lax.broadcasted_iota(jnp.int32, (rows, rows), 0)
-    column_at = lax.broadcasted_iota(jnp.int32, (rows, rows), 1)
+    out_weight = out_w_ref[...].astype(jnp.float32)[None, :]
+    row_at = lax.broadcasted_iota(jnp.int32, (rows, 2 * half), 0)
+    column_at = lax.broadcasted_iota(jnp.int32, (rows, 2 * half), 1)
     spares = pieces - tables
 
     for c in range(CHUNKS):
@@ -219,16 +219,16 @@
         if c == 0:
             load_v.wait()
             load_w.wait()
-        pre_act = b1_ref[...]
+        pre_act = b1_ref[...][None, :]
         for part in parts:
-            cross_out = dot(low_rank, v_ref[:, part]) + bias_ref[:, part]
+            cross_out = dot(low_rank, v_ref[:, part]) + bias_ref[part][None, :]
             crossed[:, part] = cross_out
             own = feats[:, part]
             pre_act = pre_act + dot((own * cross_out + own).astype(jnp.bfloat16), w_ref[part, :])
         sig_act = jax.nn.sigmoid(pre_act)
         logits = jnp.sum(pre_act * sig_act * out_weight, axis=1, keepdims=True)
         labels = jnp.sum(
-            jnp.where(row_at == column_at, label_ref[pl.ds(role * CHUNKS + c, 1), :], 0.0),
+            jnp.where(row_at + (role * half + c * rows) == column_at, label_ref[...][None, :], 0.0),
             axis=1,
             keepdims=True,
         )
@@ -297,8 +297,8 @@
             vmem_limit_bytes=56 * 1024 * 1024, collective_id=0, has_side_effects=True
         ),
     )(
-        piece_table, *chosen, pooled, dense_input, labels.reshape(2 * CHUNKS, rows), cross_bias[None],
-        top_b1[None], out_w[None], cross_u, cross_v, top_w1,
+        piece_table, *chosen, pooled, dense_input, labels, cross_bias,
+        top_b1, out_w, cross_u, cross_v, top_w1,
     )
 
 

time: 97.8 us -> 93.5 us (0.956); the launches traced: 99.1 us -> 92.5 us
  local copies, waits for them, and re-layouts: 14.1 us -> 10.2 us
  Pallas kernels: 83.8 us -> 81 us
    pallas_call x1, Pallas kernels: 62 us -> 59.2 us  [dense(): pl.pallas_call(dense_kernel, out_shape=jax.ShapeDtypeStruct(pooled.shape,...]
    broadcast_in_dim x2 -> x0, local copies, waits for them, and re-layouts: 2.6 us -> none  [the longest x1 1.33 us: dense(): cross_bias[None]]
    reshape x1 -> x0, local copies, waits for them, and re-layouts: 1.32 us -> none  [dense(): labels.reshape(2 * CHUNKS, rows)]
where the time goes in v1:
time: 93.5 us; the launch traced here: 92.5 us
  Pallas kernels  81 us (87%)
  local copies, waits for them, and re-layouts  10.2 us (11%)
  other arithmetic  1.26 us (1%)
    pallas_call x1, Pallas kernels, dense(): pl.pallas_call(dense_kernel, out_shape=jax.ShapeDtypeStruct(pooled.shape,...  59.2 us
    pallas_call x1, Pallas kernels, pool(): pl.pallas_call(pool_kernel, out_shape=[jax.ShapeDtypeStruct((blocks, piec...  21.8 us
    unnamed x18, local copies, waits for them, and re-layouts  6.9 us
    transpose x1, local copies, waits for them, and re-layouts, local(): return returned.transpose(0, 2, 1, 3)  3.28 us

profile of v1, /device:TPU:0, one launch (start us, length us, event | category | flops | bytes accessed | tf_op | source)
XLA Modules:
  0.0 92.5 jit_solution(2174885908895628423)
XLA Ops:
  0.0 1.3 %convert_reduce_fusion = (s32[2,16]{1,0:T(2,128)S(1)}, s32[2,16]{1,0:T(2,128)S(1)}) fusion(s32[2,8192]{1,0:T(2,128)} %bags_ref.1, s32[16]{0:T(128)S(1)} %get-tuple-element.16, s32[16]{0:T(128)S(1)} %get-tuple-element.15), kind=kLoop, calls=%fused_computation | loop fusion | flops 1572800 | bytes 65920 | tf_op jit(solution)/shard_map/reduce_sum | solution.py:104
  1.3 0.0 copy-start.1
  1.3 1.2 %copy-done.1 = bf16[2,2048,128]{2,1,0:T(8,128)(2,1)S(1)} copy-done((bf16[2,2048,128]{2,1,0:T(8,128)(2,1)S(1)}, bf16[2,2048,128]{2,1,0:T(8,128)(2,1)}, u32[]{:S(2)}) %copy-start.1) | copy-done | bytes 1048600
  2.5 0.0 copy-start.2
  2.5 0.8 copy-done.2
  3.3 0.0 copy-start.3
  3.3 0.8 copy-done.3
  4.2 0.0 copy-start.4
  4.2 0.8 copy-done.4
  4.9 0.0 copy-start.5
  4.9 0.7 copy-done.5
  5.6 21.8 %shard_map.127 = (bf16[16,2,128,128]{3,2,1,0:T(8,128)(2,1)S(1)}, s32[26]{0:T(128)S(1)}, s32[6]{0:T(128)S(1)}, s32[6]{0:T(128)S(1)}) custom-call(s32[32]{0:T(128)S(1)} %copy-done.5, s32[2,16]{1,0:T(2,128)S(1)} %get-tuple-element.14.first_ref, s32[2,16]{1,0:T(2,128)S(1)} %get-tuple-element.13.last_ref, bf16[2,2048,128]{2,1,0:T(8,128)(2,1)S(1)} %copy-done.1, ...), custom_call_target="tpu_custom_call" | custom-call | tf_op jit(solution)/shard_map/pallas_call | solution.py:108
  27.4 0.0 copy-start
  27.4 1.0 %copy-done = bf16[16,2,128,128]{3,2,1,0:T(8,128)(2,1)} copy-done((bf16[16,2,128,128]{3,2,1,0:T(8,128)(2,1)}, bf16[16,2,128,128]{3,2,1,0:T(8,128)(2,1)S(1)}, u32[]{:S(2)}) %copy-start) | copy-done | bytes 1048600
  28.4 0.0 copy-start.6
  28.4 0.5 copy-done.6
  28.9 0.0 copy-start.7
  28.9 0.6 copy-done.7
  29.5 0.0 copy-start.8
  29.5 0.5 copy-done.8
  30.0 59.2 %shard_map.128 = bf16[16,2,128,128]{3,2,1,0:T(8,128)(2,1)} custom-call(s32[32]{0:T(128)} %owner_ref.3, s32[26]{0:T(128)} %copy-done.6, s32[6]{0:T(128)} %copy-done.7, s32[6]{0:T(128)} %copy-done.8, bf16[16,2,128,128]{3,2,1,0:T(8,128)(2,1)} %copy-done, bf16[256,128]{1,0:T(8,128)(2,1)} %dense_ref.1, f32[256]{0:T(256)} %label_ref.1, f32[3456]{0:T(1024)} %bias_ref.1, ...), custom_call_target="tpu_custom_call" | custom-call | tf_op jit(solution)/shard_map/pallas_call | solution.py:278
  89.2 3.3 %copy.15 = bf16[16,128,2,128]{3,2,1,0:T(2,128)(2,1)} copy(bf16[16,128,2,128]{3,1,2,0:T(8,128)(2,1)} %bitcast.1) | data formatting | bytes 2097152 | tf_op jit(solution)/shard_map/transpose | solution.py:316
  (1 shorter events, 0.0 us)
Async XLA Ops:
  1.3 1.2 %copy-start.1 = (bf16[2,2048,128]{2,1,0:T(8,128)(2,1)S(1)}, bf16[2,2048,128]{2,1,0:T(8,128)(2,1)}, u32[]{:S(2)}) copy-start(bf16[2,2048,128]{2,1,0:T(8,128)(2,1)} %table_ref.1) | copy-start | bytes 3145732
  2.5 0.8 copy-start.2
  3.3 0.8 copy-start.3
  4.2 0.8 copy-start.4
  4.9 0.7 copy-start.5
  27.4 1.0 %copy-start = (bf16[16,2,128,128]{3,2,1,0:T(8,128)(2,1)}, bf16[16,2,128,128]{3,2,1,0:T(8,128)(2,1)S(1)}, u32[]{:S(2)}) copy-start(bf16[16,2,128,128]{3,2,1,0:T(8,128)(2,1)S(1)} %get-tuple-element.12.pooled_ref) | copy-start | bytes 3145732
  28.4 0.5 copy-start.6
  28.9 0.6 copy-start.7
  29.5 0.5 copy-start.8
